TPU v7x, 32 devices: a whole 2x2x4 slice. The times are simulated.
32 devices in a mesh: row: 16 (over z, y, core), col: 2 (over x).
Axes of the slice: x: 2, y: 2, z: 4, core: 2. Of those that a mesh axis runs over, the one named last changes fastest.
Arguments:
- start: float32 [32768, 128], P(('row', 'col')), may hold values from -18 to 18
- couplings: bfloat16 [128, 5, 256, 256], P(('row', 'col')), may hold values from -0.15625 to 0.15625
- tile_cols: int32 [128, 5], P(('row', 'col')), may hold values from 0 to 19
- stiffness: float32 [32768], P(('row', 'col')), may hold values from 1.5 to 4
- masses: float32 [32768], P(('row', 'col')), may hold values from 0.8 to 2.5, as said below
- bounds: float32 [2], replicated, may hold values from 1.8 to 6.5, as said below
Outputs:
- basis: float32 [32768, 128], P(('row', 'col'))
- ritz: float32 [128, 128], replicated
Inputs may be any that keep to these rules, and one draw needn't show every extreme that they name: Positive masses. bounds[0] < bounds[1].
All inputs are finite; a program needn't handle non-finite values.
Results may differ from a plain program's by a relative error of at most 0.0014.
Values may be sent and summed in bfloat16 or wider, within the bound.
No kernel may reach another device: no remote copies, remote signals or barrier semaphores. Data moves between devices by JAX's collectives and lax.ppermute only.
A program may use at most 64 MiB of HBM per device.

v0:
```python
import jax
import jax.numpy as jnp
from jax import lax
from jax.sharding import PartitionSpec as P

DEGREE = 8


def with_halo(cells, sides, width):
    for axis, dim in sides:
        count = lax.axis_size(axis)
        ends = count - 1
        head = lax.slice_in_dim(cells, 0, width, axis=dim)
        tail = lax.slice_in_dim(cells, cells.shape[dim] - width, cells.shape[dim], axis=dim)
        cells = jnp.concatenate(
            [
                lax.ppermute(tail, axis, [(i, (i + 1) % count) for i in range(ends)]),
                cells,
                lax.ppermute(head, axis, [((i + 1) % count, i) for i in range(ends)]),
            ],
            axis=dim,
        )
    return cells


def matmul_high(left, right):
    return jnp.dot(left, right, precision=lax.Precision.HIGHEST, preferred_element_type=jnp.float32)


def cholesky_inverse(gram, identity):
    factor = jnp.linalg.cholesky(gram)
    return lax.linalg.triangular_solve(factor, identity, left_side=True, lower=True)


def per_device(start, couplings, tile_cols, stiffness, masses, bounds):
    rows_dev, vec_width = start.shape
    per_block = couplings.shape[0]
    tile_size = couplings.shape[2]
    node_count = rows_dev * lax.axis_size("row") * lax.axis_size("col")

    def coupled(vectors):
        rounded = vectors.astype(jnp.bfloat16)
        line = lax.all_gather(rounded[None], "col", axis=0, tiled=True)
        column_pad = with_halo(rounded[None], (("row", 0),), 1)
        here = lax.axis_index("col")
        count = lax.axis_size("col")
        left = lax.dynamic_index_in_dim(line, jnp.maximum(here - 1, 0), 0, keepdims=False)
        right = lax.dynamic_index_in_dim(line, jnp.minimum(here + 1, count - 1), 0, keepdims=False)
        left = jnp.where(here > 0, left, jnp.zeros_like(left))
        right = jnp.where(here < count - 1, right, jnp.zeros_like(right))
        sides = [rounded, column_pad[0], column_pad[2], left, right]
        stack = jnp.stack(sides).reshape(5 * per_block, tile_size, vec_width)
        picked = stack[tile_cols]
        products = jnp.einsum(
            "psab,psbk->pak", couplings, picked, preferred_element_type=jnp.float32
        )
        return products.reshape(rows_dev, vec_width)

    stiff_column = stiffness[:, None]
    inverse_mass = 1.0 / masses[:, None]

    def stiff(vectors):
        return stiff_column * vectors - coupled(vectors)

    cut_low = bounds[0]
    cut_high = bounds[1]
    center = 0.5 * (cut_high + cut_low)
    radius = 0.5 * (cut_high - cut_low)
    scale_first = -radius / center
    twice_inverse = 2.0 / scale_first
    previous = start
    current = scale_first / radius * (stiff(start) * inverse_mass - center * start)
    scale_now = scale_first
    for iteration in range(DEGREE - 1):
        scale_next = 1.0 / (twice_inverse - scale_now)
        following = (
            2.0 * scale_next / radius * (stiff(current) * inverse_mass - center * current)
            - scale_now * scale_next * previous
        )
        previous, current, scale_now = (current, following, scale_next)
    weighted = masses[:, None] / node_count
    identity = jnp.eye(vec_width, dtype=jnp.float32)
    gram_local = matmul_high(current.T, weighted * current)
    gram = lax.psum(gram_local, ("row", "col"))
    projected = lax.psum(matmul_high(current.T, stiff(current) / node_count), ("row", "col"))
    inverse = cholesky_inverse(gram, identity)
    basis = matmul_high(current, inverse.T)
    ritz = matmul_high(matmul_high(inverse, projected), inverse.T)
    return (basis, ritz)


def solution(mesh):
    return jax.shard_map(
        per_device,
        mesh=mesh,
        in_specs=(
            P(("row", "col"), None),
            P(("row", "col"), None, None, None),
            P(("row", "col"), None),
            P(("row", "col")),
            P(("row", "col")),
            P(),
        ),
        out_specs=(P(("row", "col"), None), P()),
        check_vma=False,
    )
```

profile of v0, /device:TPU:0, one launch (start us, length us, event | category | flops | bytes accessed | tf_op | source)
XLA Modules:
  0.0 429.3 jit_solution(4073234901786170040)
XLA Ops:
  18.3 8.2 %all-gather = bf16[2048,128]{1,0:T(8,128)(2,1)S(1)} all-gather(bf16[1024,128]{1,0:T(8,128)(2,1)S(1)} %get-tuple-element.17), channel_id=2, replica_groups=mesh['row'=16,'col'=2] {'col'}, dimensions={0}, use_global_device_ids=true | all-gather | bytes 786432 | tf_op jit(solution)/shard_map/all_gather | solution.py:43
  29.5 3.2 gather_fusion
  40.0 4.4 %collective-permute-start.2 = (bf16[1,1024,128]{2,1,0:T(8,128)(2,1)S(1)}, bf16[1,1024,128]{2,1,0:T(8,128)(2,1)}, u32[]{:S(2)}, u32[]{:S(2)}) collective-permute-start(bf16[1,1024,128]{2,1,0:T(8,128)(2,1)S(1)} %bitcast.273), channel_id=1, source_target_pairs={{0,2},{2,4},{4,6},{6,8},{8,10},{10,12},{12,14},{14,16},{16,18},{18... | collective-permute-start | bytes 786440 | tf_op jit(solution)/shard_map/ppermute | solution.py:17
  45.8 7.2 %all-gather.1 = bf16[2048,128]{1,0:T(8,128)(2,1)S(1)} all-gather(bf16[1024,128]{1,0:T(8,128)(2,1)S(1)} %get-tuple-element.23), channel_id=3, replica_groups=mesh['row'=16,'col'=2] {'col'}, dimensions={0}, use_global_device_ids=true | all-gather | bytes 786432 | tf_op jit(solution)/shard_map/all_gather | solution.py:43
  57.9 3.2 gather_fusion.1
  68.7 5.1 %collective-permute-start.4 = (bf16[1,1024,128]{2,1,0:T(8,128)(2,1)S(1)}, bf16[1,1024,128]{2,1,0:T(8,128)(2,1)}, u32[]{:S(2)}, u32[]{:S(2)}) collective-permute-start(bf16[1,1024,128]{2,1,0:T(8,128)(2,1)S(1)} %bitcast.269), channel_id=1, source_target_pairs={{0,2},{2,4},{4,6},{6,8},{8,10},{10,12},{12,14},{14,16},{16,18},{18... | collective-permute-start | bytes 786440 | tf_op jit(solution)/shard_map/ppermute | solution.py:17
  75.2 7.0 %all-gather.2 = bf16[2048,128]{1,0:T(8,128)(2,1)S(1)} all-gather(bf16[1024,128]{1,0:T(8,128)(2,1)S(1)} %get-tuple-element.15), channel_id=4, replica_groups=mesh['row'=16,'col'=2] {'col'}, dimensions={0}, use_global_device_ids=true | all-gather | bytes 786432 | tf_op jit(solution)/shard_map/all_gather | solution.py:43
  87.2 3.2 gather_fusion.2
  90.3 3.1 convolution_bitcast_fusion.6
  98.1 5.2 %collective-permute-start.6 = (bf16[1,1024,128]{2,1,0:T(8,128)(2,1)S(1)}, bf16[1,1024,128]{2,1,0:T(8,128)(2,1)S(1)}, u32[]{:S(2)}, u32[]{:S(2)}) collective-permute-start(bf16[1,1024,128]{2,1,0:T(8,128)(2,1)S(1)} %bitcast.275), channel_id=1, source_target_pairs={{0,2},{2,4},{4,6},{6,8},{8,10},{10,12},{12,14},{14,16},{16,18},{18... | collective-permute-start | bytes 786440 | tf_op jit(solution)/shard_map/ppermute | solution.py:17
  104.7 7.0 %all-gather.3 = bf16[2048,128]{1,0:T(8,128)(2,1)S(1)} all-gather(bf16[1024,128]{1,0:T(8,128)(2,1)S(1)} %get-tuple-element.13), channel_id=5, replica_groups=mesh['row'=16,'col'=2] {'col'}, dimensions={0}, use_global_device_ids=true | all-gather | bytes 786432 | tf_op jit(solution)/shard_map/all_gather | solution.py:43
  114.8 3.2 gather_fusion.3
  125.6 6.0 %collective-permute-start.8 = (bf16[1,1024,128]{2,1,0:T(8,128)(2,1)S(1)}, bf16[1,1024,128]{2,1,0:T(8,128)(2,1)S(1)}, u32[]{:S(2)}, u32[]{:S(2)}) collective-permute-start(bf16[1,1024,128]{2,1,0:T(8,128)(2,1)S(1)} %bitcast.277), channel_id=1, source_target_pairs={{0,2},{2,4},{4,6},{6,8},{8,10},{10,12},{12,14},{14,16},{16,18},{18... | collective-permute-start | bytes 786440 | tf_op jit(solution)/shard_map/ppermute | solution.py:17
  133.0 7.0 %all-gather.4 = bf16[2048,128]{1,0:T(8,128)(2,1)S(1)} all-gather(bf16[1024,128]{1,0:T(8,128)(2,1)S(1)} %get-tuple-element.11), channel_id=6, replica_groups=mesh['row'=16,'col'=2] {'col'}, dimensions={0}, use_global_device_ids=true | all-gather | bytes 786432 | tf_op jit(solution)/shard_map/all_gather | solution.py:43
  143.0 3.2 gather_fusion.4
  151.9 6.7 %collective-permute-start.10 = (bf16[1,1024,128]{2,1,0:T(8,128)(2,1)S(1)}, bf16[1,1024,128]{2,1,0:T(8,128)(2,1)}, u32[]{:S(2)}, u32[]{:S(2)}) collective-permute-start(bf16[1,1024,128]{2,1,0:T(8,128)(2,1)S(1)} %bitcast.279), channel_id=1, source_target_pairs={{0,2},{2,4},{4,6},{6,8},{8,10},{10,12},{12,14},{14,16},{16,18},{18... | collective-permute-start | bytes 786440 | tf_op jit(solution)/shard_map/ppermute | solution.py:17
  160.0 7.0 %all-gather.5 = bf16[2048,128]{1,0:T(8,128)(2,1)S(1)} all-gather(bf16[1024,128]{1,0:T(8,128)(2,1)S(1)} %get-tuple-element.9), channel_id=7, replica_groups=mesh['row'=16,'col'=2] {'col'}, dimensions={0}, use_global_device_ids=true | all-gather | bytes 786432 | tf_op jit(solution)/shard_map/all_gather | solution.py:43
  172.0 3.2 gather_fusion.5
  175.2 3.1 convolution_bitcast_fusion.3
  182.8 6.0 %collective-permute-start.12 = (bf16[1,1024,128]{2,1,0:T(8,128)(2,1)S(1)}, bf16[1,1024,128]{2,1,0:T(8,128)(2,1)}, u32[]{:S(2)}, u32[]{:S(2)}) collective-permute-start(bf16[1,1024,128]{2,1,0:T(8,128)(2,1)S(1)} %bitcast.281), channel_id=1, source_target_pairs={{0,2},{2,4},{4,6},{6,8},{8,10},{10,12},{12,14},{14,16},{16,18},{18... | collective-permute-start | bytes 786440 | tf_op jit(solution)/shard_map/ppermute | solution.py:17
  190.2 7.2 %all-gather.6 = bf16[2048,128]{1,0:T(8,128)(2,1)S(1)} all-gather(bf16[1024,128]{1,0:T(8,128)(2,1)S(1)} %get-tuple-element.7), channel_id=8, replica_groups=mesh['row'=16,'col'=2] {'col'}, dimensions={0}, use_global_device_ids=true | all-gather | bytes 786432 | tf_op jit(solution)/shard_map/all_gather | solution.py:43
  202.3 3.2 gather_fusion.6
  205.5 3.1 convolution_bitcast_fusion.2
  212.9 5.3 %collective-permute-start.14 = (bf16[1,1024,128]{2,1,0:T(8,128)(2,1)S(1)}, bf16[1,1024,128]{2,1,0:T(8,128)(2,1)S(1)}, u32[]{:S(2)}, u32[]{:S(2)}) collective-permute-start(bf16[1,1024,128]{2,1,0:T(8,128)(2,1)S(1)} %bitcast.267), channel_id=1, source_target_pairs={{0,2},{2,4},{4,6},{6,8},{8,10},{10,12},{12,14},{14,16},{16,18},{18... | collective-permute-start | bytes 786440 | tf_op jit(solution)/shard_map/ppermute | solution.py:17
  219.6 7.0 %all-gather.7 = bf16[2048,128]{1,0:T(8,128)(2,1)S(1)} all-gather(bf16[1024,128]{1,0:T(8,128)(2,1)S(1)} %get-tuple-element.30), channel_id=9, replica_groups=mesh['row'=16,'col'=2] {'col'}, dimensions={0}, use_global_device_ids=true | all-gather | bytes 786432 | tf_op jit(solution)/shard_map/all_gather | solution.py:43
  229.6 3.2 gather_fusion.7
  238.0 5.2 %collective-permute-start.16 = (bf16[1,1024,128]{2,1,0:T(8,128)(2,1)S(1)}, bf16[1,1024,128]{2,1,0:T(8,128)(2,1)S(1)}, u32[]{:S(2)}, u32[]{:S(2)}) collective-permute-start(bf16[1,1024,128]{2,1,0:T(8,128)(2,1)S(1)} %bitcast.265), channel_id=1, source_target_pairs={{0,2},{2,4},{4,6},{6,8},{8,10},{10,12},{12,14},{14,16},{16,18},{18... | collective-permute-start | bytes 786440 | tf_op jit(solution)/shard_map/ppermute | solution.py:17
  246.3 7.0 %all-gather.8 = bf16[2048,128]{1,0:T(8,128)(2,1)S(1)} all-gather(bf16[1024,128]{1,0:T(8,128)(2,1)S(1)} %get-tuple-element.5), channel_id=10, replica_groups=mesh['row'=16,'col'=2] {'col'}, dimensions={0}, use_global_device_ids=true | all-gather | bytes 786432 | tf_op jit(solution)/shard_map/all_gather | solution.py:43
  254.7 3.2 gather_fusion.8
  265.9 129.1 %all-reduce.3.cloned.1.call-done = (f32[128,128]{0,1:T(8,128)}, f32[128,128]{1,0:T(8,128)}) async-done(((f32[128,128]{0,1:T(8,128)}, f32[128,128]{1,0:T(8,128)}), (f32[128,128]{0,1:T(8,128)}, f32[128,128]{1,0:T(8,128)})) %all-reduce.3.cloned.1.call-update) | async-done | bytes 131088 | tf_op jit(solution)/shard_map/psum | solution.py:84
  396.9 11.7 %cholesky.17 = f32[128,128]{1,0:T(8,128)S(1)} custom-call(f32[128,128]{1,0:T(8,128)S(1)} %fusion.38), custom_call_target="Cholesky" | custom-call | tf_op jit(solution)/shard_map/jit(cholesky)/cholesky | solution.py:31
  409.9 9.8 %custom-call.6 = f32[1,128,128]{1,2,0:T(8,128)S(1)} custom-call(f32[1,128,128]{2,1,0:T(8,128)S(1)} %fusion.35), custom_call_target="InvertDiagBlocksLowerTriangular" | custom-call | tf_op jit(solution)/shard_map/triangular_solve | solution.py:32
  (121 shorter events, 114.3 us)
Async XLA Ops:
  7.2 25.6 %copy-start = (bf16[4,5,256,256]{3,2,1,0:T(8,128)(2,1)S(1)}, bf16[4,5,256,256]{3,2,1,0:T(8,128)(2,1)}, u32[]{:S(2)}) copy-start(bf16[4,5,256,256]{3,2,1,0:T(8,128)(2,1)} %param.7) | copy-start | bytes 7864324
  7.2 387.9 %all-reduce.3.cloned.1.call-start = ((), (), s32[]{:S(2)}) async-start(), calls=%async_computation | async-start | bytes 262144 | tf_op jit(solution)/shard_map/psum | solution.py:84
  9.2 17.4 %collective-permute-start = (bf16[1,1024,128]{2,1,0:T(8,128)(2,1)S(1)}, bf16[1,1024,128]{2,1,0:T(8,128)(2,1)S(1)}, u32[]{:S(2)}, u32[]{:S(2)}) collective-permute-start(bf16[1,1024,128]{2,1,0:T(8,128)(2,1)S(1)} %bitcast.271), channel_id=1, source_target_pairs={{0,2},{2,4},{4,6},{6,8},{8,10},{10,12},{12,14},{14,16},{16,18},{18... | collective-permute-start | bytes 786440 | tf_op jit(solution)/shard_map/ppermute | solution.py:17
  11.6 15.7 %collective-permute-start.1 = (bf16[1,1024,128]{2,1,0:T(8,128)(2,1)S(1)}, bf16[1,1024,128]{2,1,0:T(8,128)(2,1)S(1)}, u32[]{:S(2)}, u32[]{:S(2)}) collective-permute-start(bf16[1,1024,128]{2,1,0:T(8,128)(2,1)S(1)} %bitcast.272), channel_id=1, source_target_pairs={{2,0},{4,2},{6,4},{8,6},{10,8},{12,10},{14,12},{16,14},{18,16},{20... | collective-permute-start | bytes 786440 | tf_op jit(solution)/shard_map/ppermute | solution.py:19
  32.7 5.2 %copy-start.5 = (f32[1024]{0:T(1024)S(1)}, f32[1024]{0:T(1024)}, u32[]{:S(2)}) copy-start(f32[1024]{0:T(1024)} %param.9) | copy-start | bytes 12292
  35.9 2.1 copy-start.1
  40.0 13.0 %collective-permute-start.2 = (bf16[1,1024,128]{2,1,0:T(8,128)(2,1)S(1)}, bf16[1,1024,128]{2,1,0:T(8,128)(2,1)}, u32[]{:S(2)}, u32[]{:S(2)}) collective-permute-start(bf16[1,1024,128]{2,1,0:T(8,128)(2,1)S(1)} %bitcast.273), channel_id=1, source_target_pairs={{0,2},{2,4},{4,6},{6,8},{8,10},{10,12},{12,14},{14,16},{16,18},{18... | collective-permute-start | bytes 786440 | tf_op jit(solution)/shard_map/ppermute | solution.py:17
  44.4 10.3 %collective-permute-start.3 = (bf16[1,1024,128]{2,1,0:T(8,128)(2,1)S(1)}, bf16[1,1024,128]{2,1,0:T(8,128)(2,1)}, u32[]{:S(2)}, u32[]{:S(2)}) collective-permute-start(bf16[1,1024,128]{2,1,0:T(8,128)(2,1)S(1)} %bitcast.274), channel_id=1, source_target_pairs={{2,0},{4,2},{6,4},{8,6},{10,8},{12,10},{14,12},{16,14},{18,16},{20... | collective-permute-start | bytes 786440 | tf_op jit(solution)/shard_map/ppermute | solution.py:19
  68.7 13.5 %collective-permute-start.4 = (bf16[1,1024,128]{2,1,0:T(8,128)(2,1)S(1)}, bf16[1,1024,128]{2,1,0:T(8,128)(2,1)}, u32[]{:S(2)}, u32[]{:S(2)}) collective-permute-start(bf16[1,1024,128]{2,1,0:T(8,128)(2,1)S(1)} %bitcast.269), channel_id=1, source_target_pairs={{0,2},{2,4},{4,6},{6,8},{8,10},{10,12},{12,14},{14,16},{16,18},{18... | collective-permute-start | bytes 786440 | tf_op jit(solution)/shard_map/ppermute | solution.py:17
  73.8 10.1 %collective-permute-start.5 = (bf16[1,1024,128]{2,1,0:T(8,128)(2,1)S(1)}, bf16[1,1024,128]{2,1,0:T(8,128)(2,1)}, u32[]{:S(2)}, u32[]{:S(2)}) collective-permute-start(bf16[1,1024,128]{2,1,0:T(8,128)(2,1)S(1)} %bitcast.270), channel_id=1, source_target_pairs={{2,0},{4,2},{6,4},{8,6},{10,8},{12,10},{14,12},{16,14},{18,16},{20... | collective-permute-start | bytes 786440 | tf_op jit(solution)/shard_map/ppermute | solution.py:19
  98.1 13.6 %collective-permute-start.6 = (bf16[1,1024,128]{2,1,0:T(8,128)(2,1)S(1)}, bf16[1,1024,128]{2,1,0:T(8,128)(2,1)S(1)}, u32[]{:S(2)}, u32[]{:S(2)}) collective-permute-start(bf16[1,1024,128]{2,1,0:T(8,128)(2,1)S(1)} %bitcast.275), channel_id=1, source_target_pairs={{0,2},{2,4},{4,6},{6,8},{8,10},{10,12},{12,14},{14,16},{16,18},{18... | collective-permute-start | bytes 786440 | tf_op jit(solution)/shard_map/ppermute | solution.py:17
  103.3 9.2 %collective-permute-start.7 = (bf16[1,1024,128]{2,1,0:T(8,128)(2,1)S(1)}, bf16[1,1024,128]{2,1,0:T(8,128)(2,1)S(1)}, u32[]{:S(2)}, u32[]{:S(2)}) collective-permute-start(bf16[1,1024,128]{2,1,0:T(8,128)(2,1)S(1)} %bitcast.276), channel_id=1, source_target_pairs={{2,0},{4,2},{6,4},{8,6},{10,8},{12,10},{14,12},{16,14},{18,16},{20... | collective-permute-start | bytes 786440 | tf_op jit(solution)/shard_map/ppermute | solution.py:19
  121.1 2.1 copy-start.3
  125.6 14.4 %collective-permute-start.8 = (bf16[1,1024,128]{2,1,0:T(8,128)(2,1)S(1)}, bf16[1,1024,128]{2,1,0:T(8,128)(2,1)S(1)}, u32[]{:S(2)}, u32[]{:S(2)}) collective-permute-start(bf16[1,1024,128]{2,1,0:T(8,128)(2,1)S(1)} %bitcast.277), channel_id=1, source_target_pairs={{0,2},{2,4},{4,6},{6,8},{8,10},{10,12},{12,14},{14,16},{16,18},{18... | collective-permute-start | bytes 786440 | tf_op jit(solution)/shard_map/ppermute | solution.py:17
  131.6 9.2 %collective-permute-start.9 = (bf16[1,1024,128]{2,1,0:T(8,128)(2,1)S(1)}, bf16[1,1024,128]{2,1,0:T(8,128)(2,1)S(1)}, u32[]{:S(2)}, u32[]{:S(2)}) collective-permute-start(bf16[1,1024,128]{2,1,0:T(8,128)(2,1)S(1)} %bitcast.278), channel_id=1, source_target_pairs={{2,0},{4,2},{6,4},{8,6},{10,8},{12,10},{14,12},{16,14},{18,16},{20... | collective-permute-start | bytes 786440 | tf_op jit(solution)/shard_map/ppermute | solution.py:19
  151.9 58.7 %copy-start.2 = (f32[1024,128]{1,0:T(8,128)}, f32[1024,128]{1,0:T(8,128)S(1)}, u32[]{:S(2)}) copy-start(f32[1024,128]{1,0:T(8,128)S(1)} %get-tuple-element.27) | copy-start | bytes 1572868
  151.9 15.2 %collective-permute-start.10 = (bf16[1,1024,128]{2,1,0:T(8,128)(2,1)S(1)}, bf16[1,1024,128]{2,1,0:T(8,128)(2,1)}, u32[]{:S(2)}, u32[]{:S(2)}) collective-permute-start(bf16[1,1024,128]{2,1,0:T(8,128)(2,1)S(1)} %bitcast.279), channel_id=1, source_target_pairs={{0,2},{2,4},{4,6},{6,8},{8,10},{10,12},{12,14},{14,16},{16,18},{18... | collective-permute-start | bytes 786440 | tf_op jit(solution)/shard_map/ppermute | solution.py:17
  158.7 10.1 %collective-permute-start.11 = (bf16[1,1024,128]{2,1,0:T(8,128)(2,1)S(1)}, bf16[1,1024,128]{2,1,0:T(8,128)(2,1)}, u32[]{:S(2)}, u32[]{:S(2)}) collective-permute-start(bf16[1,1024,128]{2,1,0:T(8,128)(2,1)S(1)} %bitcast.280), channel_id=1, source_target_pairs={{2,0},{4,2},{6,4},{8,6},{10,8},{12,10},{14,12},{16,14},{18,16},{20... | collective-permute-start | bytes 786440 | tf_op jit(solution)/shard_map/ppermute | solution.py:19
  182.8 14.6 %collective-permute-start.12 = (bf16[1,1024,128]{2,1,0:T(8,128)(2,1)S(1)}, bf16[1,1024,128]{2,1,0:T(8,128)(2,1)}, u32[]{:S(2)}, u32[]{:S(2)}) collective-permute-start(bf16[1,1024,128]{2,1,0:T(8,128)(2,1)S(1)} %bitcast.281), channel_id=1, source_target_pairs={{0,2},{2,4},{4,6},{6,8},{8,10},{10,12},{12,14},{14,16},{16,18},{18... | collective-permute-start | bytes 786440 | tf_op jit(solution)/shard_map/ppermute | solution.py:17
  188.8 10.3 %collective-permute-start.13 = (bf16[1,1024,128]{2,1,0:T(8,128)(2,1)S(1)}, bf16[1,1024,128]{2,1,0:T(8,128)(2,1)}, u32[]{:S(2)}, u32[]{:S(2)}) collective-permute-start(bf16[1,1024,128]{2,1,0:T(8,128)(2,1)S(1)} %bitcast.282), channel_id=1, source_target_pairs={{2,0},{4,2},{6,4},{8,6},{10,8},{12,10},{14,12},{16,14},{18,16},{20... | collective-permute-start | bytes 786440 | tf_op jit(solution)/shard_map/ppermute | solution.py:19
  212.9 13.7 %collective-permute-start.14 = (bf16[1,1024,128]{2,1,0:T(8,128)(2,1)S(1)}, bf16[1,1024,128]{2,1,0:T(8,128)(2,1)S(1)}, u32[]{:S(2)}, u32[]{:S(2)}) collective-permute-start(bf16[1,1024,128]{2,1,0:T(8,128)(2,1)S(1)} %bitcast.267), channel_id=1, source_target_pairs={{0,2},{2,4},{4,6},{6,8},{8,10},{10,12},{12,14},{14,16},{16,18},{18... | collective-permute-start | bytes 786440 | tf_op jit(solution)/shard_map/ppermute | solution.py:17
  218.2 9.2 %collective-permute-start.15 = (bf16[1,1024,128]{2,1,0:T(8,128)(2,1)S(1)}, bf16[1,1024,128]{2,1,0:T(8,128)(2,1)S(1)}, u32[]{:S(2)}, u32[]{:S(2)}) collective-permute-start(bf16[1,1024,128]{2,1,0:T(8,128)(2,1)S(1)} %bitcast.268), channel_id=1, source_target_pairs={{2,0},{4,2},{6,4},{8,6},{10,8},{12,10},{14,12},{16,14},{18,16},{20... | collective-permute-start | bytes 786440 | tf_op jit(solution)/shard_map/ppermute | solution.py:19
  238.0 15.3 %collective-permute-start.16 = (bf16[1,1024,128]{2,1,0:T(8,128)(2,1)S(1)}, bf16[1,1024,128]{2,1,0:T(8,128)(2,1)S(1)}, u32[]{:S(2)}, u32[]{:S(2)}) collective-permute-start(bf16[1,1024,128]{2,1,0:T(8,128)(2,1)S(1)} %bitcast.265), channel_id=1, source_target_pairs={{0,2},{2,4},{4,6},{6,8},{8,10},{10,12},{12,14},{14,16},{16,18},{18... | collective-permute-start | bytes 786440 | tf_op jit(solution)/shard_map/ppermute | solution.py:17
  243.2 10.2 %collective-permute-start.17 = (bf16[1,1024,128]{2,1,0:T(8,128)(2,1)S(1)}, bf16[1,1024,128]{2,1,0:T(8,128)(2,1)S(1)}, u32[]{:S(2)}, u32[]{:S(2)}) collective-permute-start(bf16[1,1024,128]{2,1,0:T(8,128)(2,1)S(1)} %bitcast.266), channel_id=1, source_target_pairs={{2,0},{4,2},{6,4},{8,6},{10,8},{12,10},{14,12},{16,14},{18,16},{20... | collective-permute-start | bytes 786440 | tf_op jit(solution)/shard_map/ppermute | solution.py:19
  253.6 1.1 copy-start.4
  395.0 26.3 %copy-start.6 = (f32[128,128]{1,0:T(8,128)S(1)}, f32[128,128]{1,0:T(8,128)}, u32[]{:S(2)}) copy-start(f32[128,128]{1,0:T(8,128)} %get-tuple-element.3) | copy-start | bytes 196612
Sparse Core Ops, SparseCore 0:
  266.0 128.9 all-reduce.2
where the time goes:
time: 432 us; the launch traced here: 429 us
  waiting for transfers between devices  129 us (30%)
  local copies, waits for them, and re-layouts  67.9 us (16%)
  blocking collectives  64.9 us (15%)
  other arithmetic  59.2 us (14%)
  starting transfers between devices  57.9 us (13%)
  matrix products  32.6 us (8%)
  between operations  17.6 us (4%)
    psum x1, waiting for transfers between devices, per_device(): gram = lax.psum(gram_local, ('row', 'col'))  129 us
    all_gather x9, blocking collectives, coupled(): line = lax.all_gather(rounded[None], 'col', axis=0, tiled=True)  64.9 us
    ppermute x9, starting transfers between devices, with_halo(): lax.ppermute(tail, axis, [(i, (i + 1) % count) for i in range(ends)])  46.3 us
    gather x9, local copies, waits for them, and re-layouts, coupled(): picked = stack[tile_cols]  28.6 us
    unnamed x18, other arithmetic  26.7 us
    dot_general x9, matrix products, coupled(): jnp.einsum('psab,psbk->pak', couplings, picked, preferred_element_type=jn...  26.4 us
    unnamed x32, local copies, waits for them, and re-layouts  20.4 us
    dot_general x9, local copies, waits for them, and re-layouts, coupled(): jnp.einsum('psab,psbk->pak', couplings, picked, preferred_element_type=jn...  16.6 us
  transfers between devices with their start and end apart: 19, of which 1 were waited for; matrix products, arithmetic and copies ran while one was open for 3% of the time, Pallas kernels for 0%

commit v1 on v0

--- a/solution.py
+++ b/solution.py
@@ -81,7 +81,7 @@
     weighted = masses[:, None] / node_count
     identity = jnp.eye(vec_width, dtype=jnp.float32)
     gram_local = matmul_high(current.T, weighted * current)
-    gram = lax.psum(gram_local, ("row", "col"))
+    gram = lax.psum(lax.psum(gram_local, "col"), "row")
     projected = lax.psum(matmul_high(current.T, stiff(current) / node_count), ("row", "col"))
     inverse = cholesky_inverse(gram, identity)
     basis = matmul_high(current, inverse.T)

time: 432 us -> 532 us (1.23)
  waiting for transfers between devices: 129 us -> 218 us
    psum x1 -> x3, waiting for transfers between devices: 129 us -> 218 us  [the longest x1 119 us: per_device(): lax.psum(matmul_high(current.T, stiff(current) / node_count), ('row', 'co...]
    unnamed x32 -> x30, local copies, waits for them, and re-layouts: 20.4 us -> 22.6 us
  transfers between devices with their start and end apart: 19 -> 21, of which waited for: 1 -> 3; matrix products, arithmetic and copies ran while one was open for 3% -> 8% of each run, Pallas kernels for 0% -> 0%
where the time goes in v1:
time: 532 us; the launch traced here: 528 us
  waiting for transfers between devices  218 us (41%)
  local copies, waits for them, and re-layouts  69.9 us (13%)
  blocking collectives  66.2 us (12%)
  other arithmetic  61.8 us (12%)
  starting transfers between devices  58.7 us (11%)
  matrix products  34.3 us (6%)
  between operations  19.1 us (4%)
    psum x1, waiting for transfers between devices, per_device(): lax.psum(matmul_high(current.T, stiff(current) / node_count), ('row', 'co...  119 us
    psum x2, waiting for transfers between devices, per_device(): gram = lax.psum(lax.psum(gram_local, 'col'), 'row')  98.9 us
    all_gather x9, blocking collectives, coupled(): line = lax.all_gather(rounded[None], 'col', axis=0, tiled=True)  66.2 us
    ppermute x9, starting transfers between devices, with_halo(): lax.ppermute(tail, axis, [(i, (i + 1) % count) for i in range(ends)])  47 us
    gather x9, local copies, waits for them, and re-layouts, coupled(): picked = stack[tile_cols]  28.6 us
    unnamed x18, other arithmetic  28.1 us
    dot_general x9, matrix products, coupled(): jnp.einsum('psab,psbk->pak', couplings, picked, preferred_element_type=jn...  26.4 us
    unnamed x30, local copies, waits for them, and re-layouts  22.6 us
  transfers between devices with their start and end apart: 21, of which 3 were waited for; matrix products, arithmetic and copies ran while one was open for 8% of the time, Pallas kernels for 0%

profile of v1, /device:TPU:0, one launch (start us, length us, event | category | flops | bytes accessed | tf_op | source)
XLA Modules:
  0.0 528.1 jit_solution(516226413662762454)
XLA Ops:
  19.2 8.2 %all-gather = bf16[2048,128]{1,0:T(8,128)(2,1)S(1)} all-gather(bf16[1024,128]{1,0:T(8,128)(2,1)S(1)} %get-tuple-element.15), channel_id=2, replica_groups=mesh['row'=16,'col'=2] {'col'}, dimensions={0}, use_global_device_ids=true | all-gather | bytes 786432 | tf_op jit(solution)/shard_map/all_gather | solution.py:43
  30.4 3.2 gather_fusion
  40.9 4.3 collective-permute-start.2
  46.7 7.2 %all-gather.1 = bf16[2048,128]{1,0:T(8,128)(2,1)S(1)} all-gather(bf16[1024,128]{1,0:T(8,128)(2,1)S(1)} %get-tuple-element.21), channel_id=3, replica_groups=mesh['row'=16,'col'=2] {'col'}, dimensions={0}, use_global_device_ids=true | all-gather | bytes 786432 | tf_op jit(solution)/shard_map/all_gather | solution.py:43
  58.7 3.2 gather_fusion.1
  69.5 5.1 collective-permute-start.4
  76.0 7.0 %all-gather.2 = bf16[2048,128]{1,0:T(8,128)(2,1)S(1)} all-gather(bf16[1024,128]{1,0:T(8,128)(2,1)S(1)} %get-tuple-element.13), channel_id=4, replica_groups=mesh['row'=16,'col'=2] {'col'}, dimensions={0}, use_global_device_ids=true | all-gather | bytes 786432 | tf_op jit(solution)/shard_map/all_gather | solution.py:43
  87.9 3.2 gather_fusion.2
  98.8 5.2 collective-permute-start.6
  105.5 7.0 %all-gather.3 = bf16[2048,128]{1,0:T(8,128)(2,1)S(1)} all-gather(bf16[1024,128]{1,0:T(8,128)(2,1)S(1)} %get-tuple-element.11), channel_id=5, replica_groups=mesh['row'=16,'col'=2] {'col'}, dimensions={0}, use_global_device_ids=true | all-gather | bytes 786432 | tf_op jit(solution)/shard_map/all_gather | solution.py:43
  115.5 3.2 gather_fusion.3
  126.3 6.0 %collective-permute-start.8 = (bf16[1,1024,128]{2,1,0:T(8,128)(2,1)S(1)}, bf16[1,1024,128]{2,1,0:T(8,128)(2,1)S(1)}, u32[]{:S(2)}, u32[]{:S(2)}) collective-permute-start(bf16[1,1024,128]{2,1,0:T(8,128)(2,1)S(1)} %bitcast.277), channel_id=1, source_target_pairs={{0,2},{2,4},{4,6},{6,8},{8,10},{10,12},{12,14},{14,16},{16,18},{18... | collective-permute-start | bytes 786440 | tf_op jit(solution)/shard_map/ppermute | solution.py:17
  133.7 7.0 %all-gather.4 = bf16[2048,128]{1,0:T(8,128)(2,1)S(1)} all-gather(bf16[1024,128]{1,0:T(8,128)(2,1)S(1)} %get-tuple-element.9), channel_id=6, replica_groups=mesh['row'=16,'col'=2] {'col'}, dimensions={0}, use_global_device_ids=true | all-gather | bytes 786432 | tf_op jit(solution)/shard_map/all_gather | solution.py:43
  143.7 3.2 gather_fusion.4
  152.6 6.7 %collective-permute-start.10 = (bf16[1,1024,128]{2,1,0:T(8,128)(2,1)S(1)}, bf16[1,1024,128]{2,1,0:T(8,128)(2,1)}, u32[]{:S(2)}, u32[]{:S(2)}) collective-permute-start(bf16[1,1024,128]{2,1,0:T(8,128)(2,1)S(1)} %bitcast.279), channel_id=1, source_target_pairs={{0,2},{2,4},{4,6},{6,8},{8,10},{10,12},{12,14},{14,16},{16,18},{18... | collective-permute-start | bytes 786440 | tf_op jit(solution)/shard_map/ppermute | solution.py:17
  160.7 7.0 %all-gather.5 = bf16[2048,128]{1,0:T(8,128)(2,1)S(1)} all-gather(bf16[1024,128]{1,0:T(8,128)(2,1)S(1)} %get-tuple-element.7), channel_id=7, replica_groups=mesh['row'=16,'col'=2] {'col'}, dimensions={0}, use_global_device_ids=true | all-gather | bytes 786432 | tf_op jit(solution)/shard_map/all_gather | solution.py:43
  172.6 3.2 gather_fusion.5
  175.8 3.1 convolution_bitcast_fusion.3
  183.4 6.0 %collective-permute-start.12 = (bf16[1,1024,128]{2,1,0:T(8,128)(2,1)S(1)}, bf16[1,1024,128]{2,1,0:T(8,128)(2,1)}, u32[]{:S(2)}, u32[]{:S(2)}) collective-permute-start(bf16[1,1024,128]{2,1,0:T(8,128)(2,1)S(1)} %bitcast.281), channel_id=1, source_target_pairs={{0,2},{2,4},{4,6},{6,8},{8,10},{10,12},{12,14},{14,16},{16,18},{18... | collective-permute-start | bytes 786440 | tf_op jit(solution)/shard_map/ppermute | solution.py:17
  190.8 7.2 %all-gather.6 = bf16[2048,128]{1,0:T(8,128)(2,1)S(1)} all-gather(bf16[1024,128]{1,0:T(8,128)(2,1)S(1)} %get-tuple-element.5), channel_id=8, replica_groups=mesh['row'=16,'col'=2] {'col'}, dimensions={0}, use_global_device_ids=true | all-gather | bytes 786432 | tf_op jit(solution)/shard_map/all_gather | solution.py:43
  202.9 3.2 gather_fusion.6
  213.5 5.3 %collective-permute-start.14 = (bf16[1,1024,128]{2,1,0:T(8,128)(2,1)S(1)}, bf16[1,1024,128]{2,1,0:T(8,128)(2,1)S(1)}, u32[]{:S(2)}, u32[]{:S(2)}) collective-permute-start(bf16[1,1024,128]{2,1,0:T(8,128)(2,1)S(1)} %bitcast.267), channel_id=1, source_target_pairs={{0,2},{2,4},{4,6},{6,8},{8,10},{10,12},{12,14},{14,16},{16,18},{18... | collective-permute-start | bytes 786440 | tf_op jit(solution)/shard_map/ppermute | solution.py:17
  220.2 7.0 %all-gather.7 = bf16[2048,128]{1,0:T(8,128)(2,1)S(1)} all-gather(bf16[1024,128]{1,0:T(8,128)(2,1)S(1)} %get-tuple-element.28), channel_id=9, replica_groups=mesh['row'=16,'col'=2] {'col'}, dimensions={0}, use_global_device_ids=true | all-gather | bytes 786432 | tf_op jit(solution)/shard_map/all_gather | solution.py:43
  230.2 3.2 gather_fusion.7
  241.2 5.9 %collective-permute-start.16 = (bf16[1,1024,128]{2,1,0:T(8,128)(2,1)S(1)}, bf16[1,1024,128]{2,1,0:T(8,128)(2,1)}, u32[]{:S(2)}, u32[]{:S(2)}) collective-permute-start(bf16[1,1024,128]{2,1,0:T(8,128)(2,1)S(1)} %bitcast.265), channel_id=1, source_target_pairs={{0,2},{2,4},{4,6},{6,8},{8,10},{10,12},{12,14},{14,16},{16,18},{18... | collective-permute-start | bytes 786440 | tf_op jit(solution)/shard_map/ppermute | solution.py:17
  248.3 17.6 %all-reduce.4.cloned.1.call-done = f32[128,128]{0,1:T(8,128)} async-done(((f32[128,128]{0,1:T(8,128)}), f32[128,128]{0,1:T(8,128)}) %all-reduce.4.cloned.1.call-update) | async-done | bytes 65552 | tf_op jit(solution)/shard_map/psum | solution.py:84
  266.0 8.4 %all-gather.8 = bf16[2048,128]{1,0:T(8,128)(2,1)} all-gather(bf16[1024,128]{1,0:T(8,128)(2,1)S(1)} %get-tuple-element.3), channel_id=10, replica_groups=mesh['row'=16,'col'=2] {'col'}, dimensions={0}, use_global_device_ids=true | all-gather | bytes 786432 | tf_op jit(solution)/shard_map/all_gather | solution.py:43
  274.4 81.3 %all-reduce.6.cloned.1.call-done = f32[128,128]{0,1:T(8,128)} async-done(((f32[128,128]{0,1:T(8,128)}), f32[128,128]{0,1:T(8,128)}) %all-reduce.6.cloned.1.call-update) | async-done | bytes 65552 | tf_op jit(solution)/shard_map/psum | solution.py:84
  357.4 11.7 %cholesky.17 = f32[128,128]{1,0:T(8,128)S(1)} custom-call(f32[128,128]{1,0:T(8,128)S(1)} %fusion.38), custom_call_target="Cholesky" | custom-call | tf_op jit(solution)/shard_map/jit(cholesky)/cholesky | solution.py:31
  370.5 10.4 %custom-call.6 = f32[1,128,128]{1,2,0:T(8,128)} custom-call(f32[1,128,128]{2,1,0:T(8,128)S(1)} %fusion.35), custom_call_target="InvertDiagBlocksLowerTriangular" | custom-call | tf_op jit(solution)/shard_map/triangular_solve | solution.py:32
  387.0 3.2 gather_fusion.8
  399.6 119.1 %all-reduce.8.cloned.1.call-done = f32[128,128]{1,0:T(8,128)} async-done(((f32[128,128]{1,0:T(8,128)}), f32[128,128]{1,0:T(8,128)}) %all-reduce.8.cloned.1.call-update) | async-done | bytes 65552 | tf_op jit(solution)/shard_map/psum | solution.py:85
  (125 shorter events, 126.4 us)
Async XLA Ops:
  8.0 25.6 %copy-start = (bf16[4,5,256,256]{3,2,1,0:T(8,128)(2,1)S(1)}, bf16[4,5,256,256]{3,2,1,0:T(8,128)(2,1)}, u32[]{:S(2)}) copy-start(bf16[4,5,256,256]{3,2,1,0:T(8,128)(2,1)} %param.7) | copy-start | bytes 7864324
  8.0 258.0 %all-reduce.4.cloned.1.call-start = ((), (), s32[]{:S(2)}) async-start(), calls=%async_computation | async-start | bytes 131072 | tf_op jit(solution)/shard_map/psum | solution.py:84
  10.0 17.4 %collective-permute-start = (bf16[1,1024,128]{2,1,0:T(8,128)(2,1)S(1)}, bf16[1,1024,128]{2,1,0:T(8,128)(2,1)S(1)}, u32[]{:S(2)}, u32[]{:S(2)}) collective-permute-start(bf16[1,1024,128]{2,1,0:T(8,128)(2,1)S(1)} %bitcast.271), channel_id=1, source_target_pairs={{0,2},{2,4},{4,6},{6,8},{8,10},{10,12},{12,14},{14,16},{16,18},{18... | collective-permute-start | bytes 786440 | tf_op jit(solution)/shard_map/ppermute | solution.py:17
  12.4 15.7 %collective-permute-start.1 = (bf16[1,1024,128]{2,1,0:T(8,128)(2,1)S(1)}, bf16[1,1024,128]{2,1,0:T(8,128)(2,1)S(1)}, u32[]{:S(2)}, u32[]{:S(2)}) collective-permute-start(bf16[1,1024,128]{2,1,0:T(8,128)(2,1)S(1)} %bitcast.272), channel_id=1, source_target_pairs={{2,0},{4,2},{6,4},{8,6},{10,8},{12,10},{14,12},{16,14},{18,16},{20... | collective-permute-start | bytes 786440 | tf_op jit(solution)/shard_map/ppermute | solution.py:19
  33.5 5.2 copy-start.5
  36.7 2.1 copy-start.1
  40.9 13.0 %collective-permute-start.2 = (bf16[1,1024,128]{2,1,0:T(8,128)(2,1)S(1)}, bf16[1,1024,128]{2,1,0:T(8,128)(2,1)}, u32[]{:S(2)}, u32[]{:S(2)}) collective-permute-start(bf16[1,1024,128]{2,1,0:T(8,128)(2,1)S(1)} %bitcast.273), channel_id=1, source_target_pairs={{0,2},{2,4},{4,6},{6,8},{8,10},{10,12},{12,14},{14,16},{16,18},{18... | collective-permute-start | bytes 786440 | tf_op jit(solution)/shard_map/ppermute | solution.py:17
  45.2 10.3 %collective-permute-start.3 = (bf16[1,1024,128]{2,1,0:T(8,128)(2,1)S(1)}, bf16[1,1024,128]{2,1,0:T(8,128)(2,1)}, u32[]{:S(2)}, u32[]{:S(2)}) collective-permute-start(bf16[1,1024,128]{2,1,0:T(8,128)(2,1)S(1)} %bitcast.274), channel_id=1, source_target_pairs={{2,0},{4,2},{6,4},{8,6},{10,8},{12,10},{14,12},{16,14},{18,16},{20... | collective-permute-start | bytes 786440 | tf_op jit(solution)/shard_map/ppermute | solution.py:19
  69.5 13.5 %collective-permute-start.4 = (bf16[1,1024,128]{2,1,0:T(8,128)(2,1)S(1)}, bf16[1,1024,128]{2,1,0:T(8,128)(2,1)}, u32[]{:S(2)}, u32[]{:S(2)}) collective-permute-start(bf16[1,1024,128]{2,1,0:T(8,128)(2,1)S(1)} %bitcast.269), channel_id=1, source_target_pairs={{0,2},{2,4},{4,6},{6,8},{8,10},{10,12},{12,14},{14,16},{16,18},{18... | collective-permute-start | bytes 786440 | tf_op jit(solution)/shard_map/ppermute | solution.py:17
  74.6 10.1 %collective-permute-start.5 = (bf16[1,1024,128]{2,1,0:T(8,128)(2,1)S(1)}, bf16[1,1024,128]{2,1,0:T(8,128)(2,1)}, u32[]{:S(2)}, u32[]{:S(2)}) collective-permute-start(bf16[1,1024,128]{2,1,0:T(8,128)(2,1)S(1)} %bitcast.270), channel_id=1, source_target_pairs={{2,0},{4,2},{6,4},{8,6},{10,8},{12,10},{14,12},{16,14},{18,16},{20... | collective-permute-start | bytes 786440 | tf_op jit(solution)/shard_map/ppermute | solution.py:19
  98.8 13.7 %collective-permute-start.6 = (bf16[1,1024,128]{2,1,0:T(8,128)(2,1)S(1)}, bf16[1,1024,128]{2,1,0:T(8,128)(2,1)S(1)}, u32[]{:S(2)}, u32[]{:S(2)}) collective-permute-start(bf16[1,1024,128]{2,1,0:T(8,128)(2,1)S(1)} %bitcast.275), channel_id=1, source_target_pairs={{0,2},{2,4},{4,6},{6,8},{8,10},{10,12},{12,14},{14,16},{16,18},{18... | collective-permute-start | bytes 786440 | tf_op jit(solution)/shard_map/ppermute | solution.py:17
  104.1 9.2 %collective-permute-start.7 = (bf16[1,1024,128]{2,1,0:T(8,128)(2,1)S(1)}, bf16[1,1024,128]{2,1,0:T(8,128)(2,1)S(1)}, u32[]{:S(2)}, u32[]{:S(2)}) collective-permute-start(bf16[1,1024,128]{2,1,0:T(8,128)(2,1)S(1)} %bitcast.276), channel_id=1, source_target_pairs={{2,0},{4,2},{6,4},{8,6},{10,8},{12,10},{14,12},{16,14},{18,16},{20... | collective-permute-start | bytes 786440 | tf_op jit(solution)/shard_map/ppermute | solution.py:19
  121.8 2.1 copy-start.3
  126.3 14.4 %collective-permute-start.8 = (bf16[1,1024,128]{2,1,0:T(8,128)(2,1)S(1)}, bf16[1,1024,128]{2,1,0:T(8,128)(2,1)S(1)}, u32[]{:S(2)}, u32[]{:S(2)}) collective-permute-start(bf16[1,1024,128]{2,1,0:T(8,128)(2,1)S(1)} %bitcast.277), channel_id=1, source_target_pairs={{0,2},{2,4},{4,6},{6,8},{8,10},{10,12},{12,14},{14,16},{16,18},{18... | collective-permute-start | bytes 786440 | tf_op jit(solution)/shard_map/ppermute | solution.py:17
  132.3 9.2 %collective-permute-start.9 = (bf16[1,1024,128]{2,1,0:T(8,128)(2,1)S(1)}, bf16[1,1024,128]{2,1,0:T(8,128)(2,1)S(1)}, u32[]{:S(2)}, u32[]{:S(2)}) collective-permute-start(bf16[1,1024,128]{2,1,0:T(8,128)(2,1)S(1)} %bitcast.278), channel_id=1, source_target_pairs={{2,0},{4,2},{6,4},{8,6},{10,8},{12,10},{14,12},{16,14},{18,16},{20... | collective-permute-start | bytes 786440 | tf_op jit(solution)/shard_map/ppermute | solution.py:19
  152.6 58.6 %copy-start.2 = (f32[1024,128]{1,0:T(8,128)}, f32[1024,128]{1,0:T(8,128)S(1)}, u32[]{:S(2)}) copy-start(f32[1024,128]{1,0:T(8,128)S(1)} %get-tuple-element.25) | copy-start | bytes 1572868
  152.6 15.1 %collective-permute-start.10 = (bf16[1,1024,128]{2,1,0:T(8,128)(2,1)S(1)}, bf16[1,1024,128]{2,1,0:T(8,128)(2,1)}, u32[]{:S(2)}, u32[]{:S(2)}) collective-permute-start(bf16[1,1024,128]{2,1,0:T(8,128)(2,1)S(1)} %bitcast.279), channel_id=1, source_target_pairs={{0,2},{2,4},{4,6},{6,8},{8,10},{10,12},{12,14},{14,16},{16,18},{18... | collective-permute-start | bytes 786440 | tf_op jit(solution)/shard_map/ppermute | solution.py:17
  159.3 10.1 %collective-permute-start.11 = (bf16[1,1024,128]{2,1,0:T(8,128)(2,1)S(1)}, bf16[1,1024,128]{2,1,0:T(8,128)(2,1)}, u32[]{:S(2)}, u32[]{:S(2)}) collective-permute-start(bf16[1,1024,128]{2,1,0:T(8,128)(2,1)S(1)} %bitcast.280), channel_id=1, source_target_pairs={{2,0},{4,2},{6,4},{8,6},{10,8},{12,10},{14,12},{16,14},{18,16},{20... | collective-permute-start | bytes 786440 | tf_op jit(solution)/shard_map/ppermute | solution.py:19
  183.4 14.6 %collective-permute-start.12 = (bf16[1,1024,128]{2,1,0:T(8,128)(2,1)S(1)}, bf16[1,1024,128]{2,1,0:T(8,128)(2,1)}, u32[]{:S(2)}, u32[]{:S(2)}) collective-permute-start(bf16[1,1024,128]{2,1,0:T(8,128)(2,1)S(1)} %bitcast.281), channel_id=1, source_target_pairs={{0,2},{2,4},{4,6},{6,8},{8,10},{10,12},{12,14},{14,16},{16,18},{18... | collective-permute-start | bytes 786440 | tf_op jit(solution)/shard_map/ppermute | solution.py:17
  189.4 10.3 %collective-permute-start.13 = (bf16[1,1024,128]{2,1,0:T(8,128)(2,1)S(1)}, bf16[1,1024,128]{2,1,0:T(8,128)(2,1)}, u32[]{:S(2)}, u32[]{:S(2)}) collective-permute-start(bf16[1,1024,128]{2,1,0:T(8,128)(2,1)S(1)} %bitcast.282), channel_id=1, source_target_pairs={{2,0},{4,2},{6,4},{8,6},{10,8},{12,10},{14,12},{16,14},{18,16},{20... | collective-permute-start | bytes 786440 | tf_op jit(solution)/shard_map/ppermute | solution.py:19
  213.5 13.7 %collective-permute-start.14 = (bf16[1,1024,128]{2,1,0:T(8,128)(2,1)S(1)}, bf16[1,1024,128]{2,1,0:T(8,128)(2,1)S(1)}, u32[]{:S(2)}, u32[]{:S(2)}) collective-permute-start(bf16[1,1024,128]{2,1,0:T(8,128)(2,1)S(1)} %bitcast.267), channel_id=1, source_target_pairs={{0,2},{2,4},{4,6},{6,8},{8,10},{10,12},{12,14},{14,16},{16,18},{18... | collective-permute-start | bytes 786440 | tf_op jit(solution)/shard_map/ppermute | solution.py:17
  218.8 9.2 %collective-permute-start.15 = (bf16[1,1024,128]{2,1,0:T(8,128)(2,1)S(1)}, bf16[1,1024,128]{2,1,0:T(8,128)(2,1)S(1)}, u32[]{:S(2)}, u32[]{:S(2)}) collective-permute-start(bf16[1,1024,128]{2,1,0:T(8,128)(2,1)S(1)} %bitcast.268), channel_id=1, source_target_pairs={{2,0},{4,2},{6,4},{8,6},{10,8},{12,10},{14,12},{16,14},{18,16},{20... | collective-permute-start | bytes 786440 | tf_op jit(solution)/shard_map/ppermute | solution.py:19
  241.1 114.5 %all-reduce.6.cloned.1.call-start = ((), (), s32[]{:S(2)}) async-start(), calls=%async_computation.1 | async-start | bytes 131072 | tf_op jit(solution)/shard_map/psum | solution.py:84
  241.2 140.9 %collective-permute-start.16 = (bf16[1,1024,128]{2,1,0:T(8,128)(2,1)S(1)}, bf16[1,1024,128]{2,1,0:T(8,128)(2,1)}, u32[]{:S(2)}, u32[]{:S(2)}) collective-permute-start(bf16[1,1024,128]{2,1,0:T(8,128)(2,1)S(1)} %bitcast.265), channel_id=1, source_target_pairs={{0,2},{2,4},{4,6},{6,8},{8,10},{10,12},{12,14},{14,16},{16,18},{18... | collective-permute-start | bytes 786440 | tf_op jit(solution)/shard_map/ppermute | solution.py:17
  247.0 136.7 %collective-permute-start.17 = (bf16[1,1024,128]{2,1,0:T(8,128)(2,1)S(1)}, bf16[1,1024,128]{2,1,0:T(8,128)(2,1)}, u32[]{:S(2)}, u32[]{:S(2)}) collective-permute-start(bf16[1,1024,128]{2,1,0:T(8,128)(2,1)S(1)} %bitcast.266), channel_id=1, source_target_pairs={{2,0},{4,2},{6,4},{8,6},{10,8},{12,10},{14,12},{16,14},{18,16},{20... | collective-permute-start | bytes 786440 | tf_op jit(solution)/shard_map/ppermute | solution.py:19
  266.0 252.7 %all-reduce.8.cloned.1.call-start = ((), (), s32[]{:S(2)}) async-start(), calls=%async_computation.2 | async-start | bytes 131072 | tf_op jit(solution)/shard_map/psum | solution.py:85
  380.9 4.5 copy-start.4
Sparse Core Ops, SparseCore 0:
  241.2 24.6 all-reduce.3
  269.4 86.1 all-reduce.5
Sparse Core Ops, SparseCore 1:
  398.3 120.4 all-reduce.7
